TPU v7x, 256 devices: a whole 4x4x8 slice. The times are simulated.
256 devices in a mesh: row: 8 (over y, z_lo), col: 8 (over z_hi, core), layer: 4 (over x).
Axes of the slice: x: 4, y: 4, z: 8 (z_hi: 4, z_lo: 2; z = z_hi * 2 + z_lo), core: 2. Of those that a mesh axis runs over, the one named last changes fastest.
Arguments:
- density_tiles: bfloat16 [192, 8, 2, 128, 128], P(('row', 'col')), may hold values from -1.5 to 1.5
- tile_columns: int32 [192, 8, 2], P(('row', 'col')), may hold values from -1 to 191, as said below
Outputs:
- square_tiles: bfloat16 [192, 8, 2, 128, 128], P(('row', 'col'), None, None, 'layer')
Inputs may be any that keep to these rules, and one draw needn't show every extreme that they name: `tile_columns`: entry [i, g, s] is a tile column in group g (columns g * 24 to (g + 1) * 24 - 1) or -1; within one block row and group the listed columns are distinct and empty slots come after the listed ones; block row i lists its own column i in the first slot of its group, whose 2 slots are all listed; other groups hold 0 to 2 listed tiles.
All inputs are finite; a program needn't handle non-finite values.
Results may differ from a plain program's by a relative error of at most 0.0048.
Values may be sent and summed in bfloat16 or wider, within the bound.
No kernel may reach another device: no remote copies, remote signals or barrier semaphores. Data moves between devices by JAX's collectives and lax.ppermute only.
A program may use at most 64 MiB of HBM per device.

v0:
```python
import jax
import jax.numpy as jnp
from jax import lax
from jax.sharding import Mesh
from jax.sharding import PartitionSpec as P

ROW = ("row_0", "row_1")
ROW_COL = ("row_0", "row_1", "col")


def filled_up(lines, devices):
    spare = -len(lines) % devices
    return jnp.pad(lines, [(0, spare)] + [(0, 0)] * (lines.ndim - 1))


def spread(array, axis, root):
    lines = jnp.where(lax.axis_index(axis) == root, array, jnp.zeros_like(array)).reshape(
        -1, *array.shape[1:][-1:]
    )
    padded = filled_up(lines, lax.axis_size(axis))
    own = lax.psum_scatter(padded, axis, scatter_dimension=0, tiled=True)
    return lax.all_gather(own, axis, axis=0, tiled=True)[: len(lines)].reshape(array.shape)


def broadcast_by_axis(array, axes, root):
    array = jnp.where(lax.axis_index(axes) == root, array, jnp.zeros_like(array))
    for axis in axes:
        array = lax.psum(array, axis)
    return array


def in_blocks(array, dim, devices):
    before, after = (array.shape[:dim], array.shape[dim + 1 :])
    return jnp.moveaxis(array.reshape(*before, devices, -1, *after), dim, 0)


def sent_and_summed(array, axis, dim):
    pieces = in_blocks(array, dim, lax.axis_size(axis))
    arrived = lax.all_to_all(pieces, axis, split_axis=0, concat_axis=0, tiled=True)
    return arrived.astype(jnp.float32).sum(axis=0)


def multiply(left_tiles, left_columns, right_tiles, right_columns, target_columns, start_row):
    is_live = left_columns >= 0
    inner_rows = jnp.where(is_live, left_columns - start_row, 0).astype(jnp.int32)
    inner_columns = right_columns[inner_rows]
    matches = (
        (inner_columns[:, :, None, :] == target_columns[:, None, :, None])
        & is_live[:, :, None, None]
        & (target_columns >= 0)[:, None, :, None]
    )
    slot_index = jnp.argmax(matches.astype(jnp.int32), axis=-1)
    located = jnp.any(matches, axis=-1)
    selected = right_tiles[inner_rows[:, :, None], slot_index]
    selected = jnp.where(located[:, :, :, None, None], selected, jnp.zeros((), jnp.bfloat16))
    return jnp.einsum("iarc,iascd->isrd", left_tiles, selected, preferred_element_type=jnp.float32)


def on_device(density_tiles, tile_columns):
    row_count = lax.axis_size(ROW)
    column_count = lax.axis_size("col")
    layer_count = lax.axis_size("layer")
    grid_tiles, grid_columns = (
        lax.all_to_all(density_tiles, "col", split_axis=1, concat_axis=0, tiled=True),
        lax.all_to_all(tile_columns, "col", split_axis=1, concat_axis=0, tiled=True),
    )
    block_tiles = grid_tiles[:, 0]
    block_columns = grid_columns[:, 0]
    group_rows = block_tiles.shape[0]
    row_ratio = column_count // row_count
    panel_rows = group_rows // row_ratio
    per_layer = column_count // layer_count
    layer_index = lax.axis_index("layer")
    partial_value = jnp.zeros(block_tiles.shape, jnp.float32)
    for panel_step in range(per_layer):
        panel_index = layer_index * per_layer + panel_step
        left_tiles, left_columns = (
            spread(block_tiles, "col", panel_index),
            spread(block_columns, "col", panel_index),
        )
        right_tiles, right_columns = (
            broadcast_by_axis(block_tiles, ROW, panel_index // row_ratio),
            broadcast_by_axis(block_columns, ROW, panel_index // row_ratio),
        )
        partial_value = partial_value + multiply(
            left_tiles,
            left_columns,
            right_tiles,
            right_columns,
            block_columns,
            panel_index * panel_rows,
        )
    rounded = partial_value.astype(jnp.bfloat16)
    summed = sent_and_summed(rounded.astype(jnp.float32).astype(jnp.bfloat16), "layer", 2)
    returned = lax.all_to_all(
        summed.astype(jnp.bfloat16)[:, None], "col", split_axis=0, concat_axis=1, tiled=True
    )
    return returned


def solution(mesh):
    split = Mesh(
        mesh.devices.reshape(4, 2, mesh.shape["col"], mesh.shape["layer"]),
        ("row_0", "row_1", "col", "layer"),
    )
    return jax.shard_map(
        on_device,
        mesh=split,
        in_specs=(P(ROW_COL, None, None, None, None), P(ROW_COL, None, None)),
        out_specs=P(ROW_COL, None, None, "layer", None),
        check_vma=False,
    )
```

profile of v0, /device:TPU:1, one launch (start us, length us, event | category | flops | bytes accessed | tf_op | source)
XLA Modules:
  0.0 319.0 jit_solution(11141987187466286460)
XLA Ops:
  7.4 2.7 copy.204
  10.1 10.0 %all-to-all-start.1 = ((bf16[3,8,2,128,128]{4,3,2,0,1:T(8,128)(2,1)}), bf16[3,8,2,128,128]{4,3,2,0,1:T(8,128)(2,1)S(1)}, u32[]{:S(2)}, u32[]{:S(2)}) async-start(bf16[3,8,2,128,128]{4,3,2,0,1:T(8,128)(2,1)} %copy.204), calls=%async_computation.1 | async-start | bytes 3145728 | tf_op jit(solution)/shard_map/all_to_all | solution.py:64
  20.1 33.3 %all-to-all-done.1 = bf16[3,8,2,128,128]{4,3,2,0,1:T(8,128)(2,1)S(1)} async-done(((bf16[3,8,2,128,128]{4,3,2,0,1:T(8,128)(2,1)}), bf16[3,8,2,128,128]{4,3,2,0,1:T(8,128)(2,1)S(1)}, u32[]{:S(2)}, u32[]{:S(2)}) %all-to-all-start.1) | async-done | bytes 1572896 | tf_op jit(solution)/shard_map/all_to_all | solution.py:64
  53.4 2.8 broadcast_select_fusion.2
  56.3 0.5 reduce-scatter.5.cloned.1.call-update
  56.8 0.5 reduce-scatter.3.cloned.1.call-update
  57.4 82.9 %all-reduce.10.cloned.1.call-done = (bf16[24,2,128,128]{3,2,1,0:T(8,128)(2,1)}, bf16[24,2,128,128]{3,2,1,0:T(8,128)(2,1)}) async-done(((bf16[24,2,128,128]{3,2,1,0:T(8,128)(2,1)}, bf16[24,2,128,128]{3,2,1,0:T(8,128)(2,1)}), (bf16[24,2,128,128]{3,2,1,0:T(8,128)(2,1)}, bf16[24,2,128,128]{3,2,1,0:T(8,128)(2,1)})) %all-reduce.10.cloned.1.call-update) | async-done | bytes 3145744 | tf_op jit(solution)/shard_map/psum | solution.py:28
  140.4 0.5 all-gather.7.cloned.1.call-update
  140.9 0.1 copy-done
  141.0 0.7 copy.187
  141.7 7.8 %all-to-all-start = ((s32[3,8,2]{0,2,1:T(2,128)}), s32[3,8,2]{0,2,1:T(2,128)S(1)}, u32[]{:S(2)}, u32[]{:S(2)}) async-start(s32[3,8,2]{0,2,1:T(2,128)} %copy.187), calls=%async_computation | async-start | bytes 16384 | tf_op jit(solution)/shard_map/all_to_all | solution.py:65
  149.5 0.6 dynamic-slice
  150.7 5.9 %all-to-all-done = s32[3,8,2]{0,2,1:T(2,128)S(1)} async-done(((s32[3,8,2]{0,2,1:T(2,128)}), s32[3,8,2]{0,2,1:T(2,128)S(1)}, u32[]{:S(2)}, u32[]{:S(2)}) %all-to-all-start) | async-done | bytes 224 | tf_op jit(solution)/shard_map/all_to_all | solution.py:65
  156.6 0.1 squeeze.4
  156.7 0.1 copy.190
  156.8 25.1 %all-reduce.2 = (s32[24,2]{1,0:T(8,128)S(1)}, s32[24,2]{1,0:T(8,128)S(1)}) all-reduce(s32[24,2]{1,0:T(8,128)S(1)} %get-tuple-element.32, s32[24,2]{1,0:T(8,128)S(1)} %get-tuple-element.34), channel_id=4, replica_groups=mesh['row_0'=4,'row_1'=2,'col'=8,'layer'=4] {'col'}, use_global_device_ids=true, to_apply=%region_10.11.clone | all-reduce | flops 96 | bytes 768
  181.9 0.1 copy.192
  182.0 12.9 %all-gather = s32[8,3,2]{1,2,0:T(2,128)S(1)} all-gather(s32[1,3,2]{1,2,0:T(2,128)S(1)} %bitcast.110), channel_id=1, replica_groups=mesh['row_0'=4,'row_1'=2,'col'=8,'layer'=4] {'col'}, dimensions={0}, use_global_device_ids=true | all-gather | bytes 216 | tf_op jit(solution)/shard_map/all_gather | solution.py:22
  194.9 0.1 copy.193
  195.1 0.1 copy.202
  195.2 0.1 copy.210
  195.3 0.1 copy.194
  195.4 0.1 reshape.112
  195.5 0.1 copy.197
  195.6 0.1 copy.196
  195.6 0.1 reshape.114
  195.7 13.0 %all-gather.1 = s32[8,3,2]{1,2,0:T(2,128)S(1)} all-gather(s32[1,3,2]{1,2,0:T(2,128)S(1)} %bitcast.109), channel_id=1, replica_groups=mesh['row_0'=4,'row_1'=2,'col'=8,'layer'=4] {'col'}, dimensions={0}, use_global_device_ids=true | all-gather | bytes 216 | tf_op jit(solution)/shard_map/all_gather | solution.py:22
  208.7 0.1 copy.211
  208.8 0.1 copy.212
  208.9 0.1 reshape.116
  209.0 0.1 copy.215
  209.1 0.1 copy.214
  209.2 0.1 reshape.118
  209.3 0.1 copy.216
  209.4 0.1 copy.220
  209.5 0.1 reshape.81
  209.6 13.5 %all-reduce.3 = (s32[24,2]{1,0:T(8,128)S(1)}, s32[24,2]{1,0:T(8,128)S(1)}) all-reduce(s32[24,2]{1,0:T(8,128)S(1)} %get-tuple-element.33, s32[24,2]{1,0:T(8,128)S(1)} %get-tuple-element.31), channel_id=1, replica_groups=mesh['row_0'=4,'row_1'=2,'col'=8,'layer'=4] {'row_0'}, use_global_device_ids=true, to_apply=%region_8.9 | all-reduce | flops 96 | bytes 768 | tf_op jit(solution)/shard_map/psum | solution.py:28
  223.0 7.7 %all-reduce.4 = (s32[24,2]{1,0:T(8,128)S(1)}, s32[24,2]{1,0:T(8,128)S(1)}) all-reduce(s32[24,2]{1,0:T(8,128)S(1)} %get-tuple-element.11, s32[24,2]{1,0:T(8,128)S(1)} %get-tuple-element.12), channel_id=1, replica_groups=mesh['row_0'=4,'row_1'=2,'col'=8,'layer'=4] {'row_1'}, use_global_device_ids=true, to_apply=%region_9.10 | all-reduce | flops 96 | bytes 768 | tf_op jit(solution)/shard_map/psum | solution.py:28
  230.7 0.6 gather_fusion.2
  231.3 0.1 copy.218
  231.4 0.1 copy.198
  231.5 0.1 copy.205
  231.6 0.1 reshape.67
  231.7 0.6 gather_fusion
  232.3 0.1 copy.200
  232.4 0.1 copy.203
  232.5 0.1 copy.219
  232.7 0.6 iota_reduce_fusion
  233.3 0.1 copy.221
  233.4 0.1 reshape.87
  233.5 0.6 iota_reduce_fusion.1
  234.2 0.1 copy.206
  234.3 0.1 reshape.73
  234.4 11.8 %all-reduce.12.cloned.1.call-done = (bf16[24,2,128,128]{3,2,1,0:T(8,128)(2,1)}, bf16[24,2,128,128]{3,2,1,0:T(8,128)(2,1)}) async-done(((bf16[24,2,128,128]{3,2,1,0:T(8,128)(2,1)}, bf16[24,2,128,128]{3,2,1,0:T(8,128)(2,1)}), (bf16[24,2,128,128]{3,2,1,0:T(8,128)(2,1)}, bf16[24,2,128,128]{3,2,1,0:T(8,128)(2,1)})) %all-reduce.12.cloned.1.call-update) | async-done | bytes 3145744 | tf_op jit(solution)/shard_map/psum | solution.py:28
  246.2 4.5 %gather_fusion.3 = bf16[96,128,128]{2,1,0:T(8,128)(2,1)} fusion(bf16[24,2,128,128]{3,2,1,0:T(8,128)(2,1)} %get-tuple-element.17, s32[96]{0:T(128)S(1)} %reshape.87), kind=kCustom, calls=%fused_computation.3 | custom fusion | bytes 6292224 | tf_op jit(solution)/shard_map/gather | solution.py:54
  250.6 3.0 gather_fusion.1
  253.7 4.8 %fusion.1 = f32[24,2,128,128,1]{2,3,1,4,0:T(8,128)} fusion(bf16[24,2,128,128,1]{3,2,4,1,0:T(8,128)(2,1)} %bitcast.105, bf16[24,2,2,128,128]{4,3,2,1,0:T(8,128)(2,1)} %bitcast.95, pred[24,2,2]{2,1,0:T(4,128)(4,1)S(1)} %copy.219), kind=kOutput, calls=%fused_computation.6 | convolution fusion | flops 404226048 | bytes 7864416 | tf_op jit(solution)/shard_map/iarc,iascd->isrd/dot_general | solution.py:56
  258.5 5.5 %all-gather.5.cloned.1.call-done = bf16[6144,128]{1,0:T(8,128)(2,1)} async-done(((bf16[768,128]{1,0:T(8,128)(2,1)}), bf16[6144,128]{1,0:T(8,128)(2,1)}) %all-gather.5.cloned.1.call-update) | async-done | bytes 1572880 | tf_op jit(solution)/shard_map/all_gather | solution.py:22
  263.9 3.0 fusion
  267.0 0.4 copy.235
  267.4 24.0 %all_to_all.47 = bf16[4,24,2,32,128]{4,3,2,1,0:T(8,128)(2,1)S(1)} all-to-all(bf16[4,24,2,32,128]{4,3,2,1,0:T(8,128)(2,1)S(1)} %bitcast.97), channel_id=1, replica_groups=mesh['row_0'=4,'row_1'=2,'col'=8,'layer'=4] {'layer'}, dimensions={0} | all-to-all | bytes 3145728 | tf_op jit(solution)/shard_map/all_to_all | solution.py:39
  291.4 0.3 reduce_sum.12
  291.8 18.9 %all_to_all.48 = bf16[24,1,2,32,128]{4,3,2,1,0:T(8,128)(2,1)S(1)} all-to-all(bf16[24,1,2,32,128]{4,3,2,1,0:T(8,128)(2,1)S(1)} %bitcast.104), channel_id=1, replica_groups=mesh['row_0'=4,'row_1'=2,'col'=8,'layer'=4] {'col'}, dimensions={0} | all-to-all | bytes 786432 | tf_op jit(solution)/shard_map/all_to_all | solution.py:95
  310.6 0.8 copy.224
  (30 shorter events, 0.4 us)
Async XLA Ops:
  10.1 43.3 %all-to-all-start.1 = ((bf16[3,8,2,128,128]{4,3,2,0,1:T(8,128)(2,1)}), bf16[3,8,2,128,128]{4,3,2,0,1:T(8,128)(2,1)S(1)}, u32[]{:S(2)}, u32[]{:S(2)}) async-start(bf16[3,8,2,128,128]{4,3,2,0,1:T(8,128)(2,1)} %copy.204), calls=%async_computation.1 | async-start | bytes 3145728 | tf_op jit(solution)/shard_map/all_to_all | solution.py:64
  20.1 120.3 %all-reduce.10.cloned.1.call-start = ((), (), s32[]{:S(2)}) async-start(), calls=%async_computation.10 | async-start | bytes 6291456 | tf_op jit(solution)/shard_map/psum | solution.py:28
  56.2 84.2 %reduce-scatter.5.cloned.1.call-start = ((), (), s32[]{:S(2)}) async-start(), calls=%async_computation.8 | async-start | bytes 1769472 | tf_op jit(solution)/shard_map/reduce_scatter | solution.py:21
  56.8 138.2 %reduce-scatter.3.cloned.1.call-start = ((), (), s32[]{:S(2)}) async-start(), calls=%async_computation.6 | async-start | bytes 1769472 | tf_op jit(solution)/shard_map/reduce_scatter | solution.py:21
  57.4 188.8 %all-reduce.12.cloned.1.call-start = ((), (), s32[]{:S(2)}) async-start(), calls=%async_computation.11 | async-start | bytes 6291456 | tf_op jit(solution)/shard_map/psum | solution.py:28
  140.3 0.7 copy-start
  140.3 9.2 %copy-start.1 = (u32[256]{0:T(256)S(1)}, u32[256]{0:T(256)}, u32[]{:S(2)}) copy-start(u32[256]{0:T(256)} %constant.100) | copy-start | bytes 3076
  140.3 113.3 %all-gather.7.cloned.1.call-start = ((), (), s32[]{:S(2)}) async-start(), calls=%async_computation.9 | async-start | bytes 1769472 | tf_op jit(solution)/shard_map/all_gather | solution.py:22
  141.7 14.9 %all-to-all-start = ((s32[3,8,2]{0,2,1:T(2,128)}), s32[3,8,2]{0,2,1:T(2,128)S(1)}, u32[]{:S(2)}, u32[]{:S(2)}) async-start(s32[3,8,2]{0,2,1:T(2,128)} %copy.187), calls=%async_computation | async-start | bytes 16384 | tf_op jit(solution)/shard_map/all_to_all | solution.py:65
  149.5 114.4 %all-gather.5.cloned.1.call-start = ((), (), s32[]{:S(2)}) async-start(), calls=%async_computation.7 | async-start | bytes 1769472 | tf_op jit(solution)/shard_map/all_gather | solution.py:22
Sparse Core Ops, SparseCore 0:
  56.3 83.9 all-reduce.9
  143.0 103.1 all-reduce.11
Sparse Core Ops, SparseCore 1:
  59.3 43.9 reduce-scatter.4
  105.7 40.1 reduce-scatter.2
  147.6 63.6 all-gather.6
  213.1 50.8 all-gather.4
where the time goes:
time: 319 us
  waiting for transfers between devices  141 us (44%)
  blocking collectives  115 us (36%)
  starting transfers between devices  18 us (6%)
  local copies, waits for them, and re-layouts  16.9 us (5%)
  between operations  15.8 us (5%)
  matrix products  7.82 us (2%)
  other arithmetic  4.51 us (1%)
    psum x2, waiting for transfers between devices, broadcast_by_axis(): array = lax.psum(array, axis)  94.7 us
    all_to_all x1, waiting for transfers between devices, on_device(): lax.all_to_all(density_tiles, 'col', split_axis=1, concat_axis=0, tiled=T...  33.3 us
    all_gather x2, blocking collectives, spread(): lax.all_gather(own, axis, axis=0, tiled=True)[:len(lines)]  25.9 us
    unnamed x1, blocking collectives  25.1 us
    all_to_all x1, blocking collectives, sent_and_summed(): lax.all_to_all(pieces, axis, split_axis=0, concat_axis=0, tiled=True)  24 us
    psum x2, blocking collectives, broadcast_by_axis(): array = lax.psum(array, axis)  21.2 us
    all_to_all x1, blocking collectives, on_device(): lax.all_to_all(summed.astype(jnp.bfloat16)[:, None], 'col', split_axis=0,...  18.9 us
    all_to_all x1, starting transfers between devices, on_device(): lax.all_to_all(density_tiles, 'col', split_axis=1, concat_axis=0, tiled=T...  9.95 us
  transfers between devices with their start and end apart: 8, of which 5 were waited for; matrix products, arithmetic and copies ran while one was open for 6% of the time, Pallas kernels for 0%

commit v1 on v0

--- a/solution.py
+++ b/solution.py
@@ -25,7 +25,7 @@
 def broadcast_by_axis(array, axes, root):
     array = jnp.where(lax.axis_index(axes) == root, array, jnp.zeros_like(array))
     for axis in axes:
-        array = lax.psum(array, axis)
+        array = jnp.sum(lax.all_gather(array, axis), axis=0)
     return array
 
 

time: 319 us -> 428 us (1.34)
  waiting for transfers between devices: 141 us -> 251 us
  blocking collectives: 115 us -> 96.8 us
  other arithmetic: 4.51 us -> 21.6 us
    all_gather x0 -> x4, waiting for transfers between devices: none -> 155 us  [broadcast_by_axis(): array = jnp.sum(lax.all_gather(array, axis), axis=0)]
    psum x2 -> x0, waiting for transfers between devices: 94.7 us -> none  [broadcast_by_axis(): array = lax.psum(array, axis)]
    all_gather x2, waiting for transfers between devices: 5.51 us -> 55 us  [spread(): lax.all_gather(own, axis, axis=0, tiled=True)[:len(lines)]]
    psum x2 -> x0, blocking collectives: 21.2 us -> none  [broadcast_by_axis(): array = lax.psum(array, axis)]
    all_gather x0 -> x4, blocking collectives: none -> 18.7 us  [broadcast_by_axis(): array = jnp.sum(lax.all_gather(array, axis), axis=0)]
    unnamed x1, blocking collectives: 25.1 us -> 7.27 us
    reduce_sum x0 -> x8, other arithmetic: none -> 17 us  [broadcast_by_axis(): array = jnp.sum(lax.all_gather(array, axis), axis=0)]
  transfers between devices with their start and end apart: 8 -> 10, of which waited for: 5 -> 7; matrix products, arithmetic and copies ran while one was open for 6% -> 8% of each run, Pallas kernels for 0% -> 0%
where the time goes in v1:
time: 428 us; the launch traced here: 427 us
  waiting for transfers between devices  251 us (59%)
  blocking collectives  96.8 us (23%)
  other arithmetic  21.6 us (5%)
  starting transfers between devices  18.1 us (4%)
  local copies, waits for them, and re-layouts  15.7 us (4%)
  between operations  15.7 us (4%)
  matrix products  7.86 us (2%)
    all_gather x4, waiting for transfers between devices, broadcast_by_axis(): array = jnp.sum(lax.all_gather(array, axis), axis=0)  155 us
    all_gather x2, waiting for transfers between devices, spread(): lax.all_gather(own, axis, axis=0, tiled=True)[:len(lines)]  55 us
    all_to_all x1, waiting for transfers between devices, on_device(): lax.all_to_all(density_tiles, 'col', split_axis=1, concat_axis=0, tiled=T...  33.3 us
    all_gather x2, blocking collectives, spread(): lax.all_gather(own, axis, axis=0, tiled=True)[:len(lines)]  27.8 us
    all_to_all x1, blocking collectives, sent_and_summed(): lax.all_to_all(pieces, axis, split_axis=0, concat_axis=0, tiled=True)  25.3 us
    all_gather x4, blocking collectives, broadcast_by_axis(): array = jnp.sum(lax.all_gather(array, axis), axis=0)  18.7 us
    all_to_all x1, blocking collectives, on_device(): lax.all_to_all(summed.astype(jnp.bfloat16)[:, None], 'col', split_axis=0,...  17.7 us
    reduce_sum x8, other arithmetic, broadcast_by_axis(): array = jnp.sum(lax.all_gather(array, axis), axis=0)  17 us
  transfers between devices with their start and end apart: 10, of which 7 were waited for; matrix products, arithmetic and copies ran while one was open for 8% of the time, Pallas kernels for 0%

profile of v1, /device:TPU:1, one launch (start us, length us, event | category | flops | bytes accessed | tf_op | source)
XLA Modules:
  0.0 427.2 jit_solution(18004346502139811795)
XLA Ops:
  7.4 2.7 copy.164
  10.1 10.0 %all-to-all-start.1 = ((bf16[3,8,2,128,128]{4,3,2,0,1:T(8,128)(2,1)}), bf16[3,8,2,128,128]{4,3,2,0,1:T(8,128)(2,1)S(1)}, u32[]{:S(2)}, u32[]{:S(2)}) async-start(bf16[3,8,2,128,128]{4,3,2,0,1:T(8,128)(2,1)} %copy.164), calls=%async_computation.1 | async-start | bytes 3145728 | tf_op jit(solution)/shard_map/all_to_all | solution.py:64
  20.1 33.3 %all-to-all-done.1 = bf16[3,8,2,128,128]{4,3,2,0,1:T(8,128)(2,1)S(1)} async-done(((bf16[3,8,2,128,128]{4,3,2,0,1:T(8,128)(2,1)}), bf16[3,8,2,128,128]{4,3,2,0,1:T(8,128)(2,1)S(1)}, u32[]{:S(2)}, u32[]{:S(2)}) %all-to-all-start.1) | async-done | bytes 1572896 | tf_op jit(solution)/shard_map/all_to_all | solution.py:64
  53.4 2.8 broadcast_select_fusion.3
  56.2 0.7 all-gather.15.cloned.1.call-update
  57.0 0.5 reduce-scatter.7.cloned.1.call-update
  57.6 0.5 reduce-scatter.5.cloned.1.call-update
  58.1 69.4 %all-gather.19.cloned.1.call-done = bf16[4,24,2,128,128]{4,3,2,1,0:T(8,128)(2,1)} async-done(((bf16[1,24,2,128,128]{4,3,2,1,0:T(8,128)(2,1)}), bf16[4,24,2,128,128]{4,3,2,1,0:T(8,128)(2,1)}) %all-gather.19.cloned.1.call-update) | async-done | bytes 6291472 | tf_op jit(solution)/shard_map/all_gather | solution.py:28
  127.6 5.7 %reduce_sum.102 = bf16[24,2,128,128]{3,2,1,0:T(8,128)(2,1)} reduce(bf16[4,24,2,128,128]{4,3,2,1,0:T(8,128)(2,1)} %all-gather.19.cloned.1.call-done, bf16[]{:T(256)} %constant.71.clone.1), dimensions={0}, to_apply=%region_12.13 | reduce | flops 2359296 | bytes 7864322 | tf_op jit(solution)/shard_map/reduce_sum | solution.py:28
  133.4 64.9 %all-gather.15.cloned.1.call-done = bf16[4,24,2,128,128]{4,3,2,1,0:T(8,128)(2,1)} async-done(((bf16[1,24,2,128,128]{4,3,2,1,0:T(8,128)(2,1)}), bf16[4,24,2,128,128]{4,3,2,1,0:T(8,128)(2,1)}) %all-gather.15.cloned.1.call-update) | async-done | bytes 6291472 | tf_op jit(solution)/shard_map/all_gather | solution.py:28
  198.3 5.7 %reduce_sum.98 = bf16[24,2,128,128]{3,2,1,0:T(8,128)(2,1)} reduce(bf16[4,24,2,128,128]{4,3,2,1,0:T(8,128)(2,1)} %all-gather.15.cloned.1.call-done, bf16[]{:T(256)} %constant.71.clone.1), dimensions={0}, to_apply=%region_4.5 | reduce | flops 2359296 | bytes 7864322 | tf_op jit(solution)/shard_map/reduce_sum | solution.py:28
  204.1 0.5 all-gather.21.cloned.1.call-update
  204.7 0.7 copy.151
  205.4 7.8 %all-to-all-start = ((s32[3,8,2]{0,2,1:T(2,128)}), s32[3,8,2]{0,2,1:T(2,128)S(1)}, u32[]{:S(2)}, u32[]{:S(2)}) async-start(s32[3,8,2]{0,2,1:T(2,128)} %copy.151), calls=%async_computation | async-start | bytes 16384 | tf_op jit(solution)/shard_map/all_to_all | solution.py:65
  213.2 0.6 dynamic-slice
  214.5 5.8 %all-to-all-done = s32[3,8,2]{0,2,1:T(2,128)S(1)} async-done(((s32[3,8,2]{0,2,1:T(2,128)}), s32[3,8,2]{0,2,1:T(2,128)S(1)}, u32[]{:S(2)}, u32[]{:S(2)}) %all-to-all-start) | async-done | bytes 224 | tf_op jit(solution)/shard_map/all_to_all | solution.py:65
  220.4 7.3 %all-reduce.2 = (s32[24,2]{0,1:T(2,128)S(1)}, s32[24,2]{0,1:T(2,128)S(1)}) all-reduce(s32[24,2]{0,1:T(2,128)S(1)} %get-tuple-element.28, s32[24,2]{0,1:T(2,128)S(1)} %get-tuple-element.27), channel_id=8, replica_groups=mesh['row_0'=4,'row_1'=2,'col'=8,'layer'=4] {'col'}, use_global_device_ids=true, to_apply=%region_10.11.clone | all-reduce | flops 96 | bytes 768
  227.7 14.1 %all-gather.5 = s32[8,3,2]{1,2,0:T(2,128)S(1)} all-gather(s32[1,3,2]{1,2,0:T(2,128)S(1)} %dynamic-slice_bitcast_fusion.1), channel_id=1, replica_groups=mesh['row_0'=4,'row_1'=2,'col'=8,'layer'=4] {'col'}, dimensions={0}, use_global_device_ids=true | all-gather | bytes 216 | tf_op jit(solution)/shard_map/all_gather | solution.py:22
  241.8 0.1 copy.155
  241.9 0.1 copy.156
  242.0 0.1 reshape.166
  242.1 0.1 copy.152
  242.2 0.1 copy.153
  242.4 6.3 %all_gather.52 = s32[4,24,2]{1,2,0:T(2,128)S(1)} all-gather(s32[1,24,2]{1,2,0:T(2,128)S(1)} %select_n.168), channel_id=1, replica_groups=mesh['row_0'=4,'row_1'=2,'col'=8,'layer'=4] {'row_0'}, dimensions={0}, use_global_device_ids=true | all-gather | bytes 960 | tf_op jit(solution)/shard_map/all_gather | solution.py:28
  248.7 3.1 all-gather.4
  251.8 0.1 copy.160
  251.9 0.1 copy.158
  252.1 0.1 copy.159
  252.2 0.1 reshape.113
  252.3 0.6 gather_fusion
  252.9 0.1 copy.162
  253.1 13.7 %all-gather.7 = s32[8,3,2]{1,2,0:T(2,128)S(1)} all-gather(s32[1,3,2]{1,2,0:T(2,128)S(1)} %dynamic-slice_bitcast_fusion), channel_id=1, replica_groups=mesh['row_0'=4,'row_1'=2,'col'=8,'layer'=4] {'col'}, dimensions={0}, use_global_device_ids=true | all-gather | bytes 216 | tf_op jit(solution)/shard_map/all_gather | solution.py:22
  266.7 0.1 copy.168
  266.8 0.1 copy.169
  266.9 0.1 reshape.170
  267.2 5.8 %all_gather.60 = s32[4,24,2]{1,2,0:T(2,128)S(1)} all-gather(s32[1,24,2]{1,2,0:T(2,128)S(1)} %select_n.187), channel_id=1, replica_groups=mesh['row_0'=4,'row_1'=2,'col'=8,'layer'=4] {'row_0'}, dimensions={0}, use_global_device_ids=true | all-gather | bytes 960 | tf_op jit(solution)/shard_map/all_gather | solution.py:28
  273.0 3.6 all-gather.6
  276.6 0.1 copy.173
  276.7 0.1 copy.171
  277.0 0.1 reshape.127
  277.1 0.6 gather_fusion.2
  277.7 0.1 copy.175
  277.8 0.6 iota_reduce_fusion
  278.5 0.1 copy.177
  278.6 0.1 reshape.133
  278.7 0.1 copy.176
  278.8 0.8 iota_reduce_fusion.1
  279.6 0.1 copy.165
  279.7 0.1 reshape.119
  279.9 0.1 copy.163
  280.0 2.8 reduce_sum.103
  282.8 20.6 %all-gather.23.cloned.1.call-done = bf16[48,2,128,128]{3,2,1,0:T(8,128)(2,1)} async-done(((bf16[24,2,128,128]{3,2,1,0:T(8,128)(2,1)}), bf16[48,2,128,128]{3,2,1,0:T(8,128)(2,1)}) %all-gather.23.cloned.1.call-update) | async-done | bytes 3145744 | tf_op jit(solution)/shard_map/all_gather | solution.py:28
  303.4 2.7 reduce_sum.99
  306.1 3.1 gather_fusion.3
  309.2 3.1 gather_fusion.1
  312.3 26.7 %all-gather.21.cloned.1.call-done = bf16[6144,128]{1,0:T(8,128)(2,1)} async-done(((bf16[768,128]{1,0:T(8,128)(2,1)}), bf16[6144,128]{1,0:T(8,128)(2,1)}) %all-gather.21.cloned.1.call-update) | async-done | bytes 1572880 | tf_op jit(solution)/shard_map/all_gather | solution.py:22
  339.1 4.8 %fusion.1 = f32[24,2,128,128,1]{2,3,1,4,0:T(8,128)} fusion(bf16[24,2,128,128,1]{3,2,4,1,0:T(8,128)(2,1)} %bitcast.128, bf16[24,2,2,128,128]{4,3,2,1,0:T(8,128)(2,1)} %bitcast.116, pred[24,2,2]{2,1,0:T(4,128)(4,1)S(1)} %copy.176), kind=kOutput, calls=%fused_computation.6 | convolution fusion | flops 404226048 | bytes 7864416 | tf_op jit(solution)/shard_map/iarc,iascd->isrd/dot_general | solution.py:56
  343.9 28.3 %all-gather.17.cloned.1.call-done = bf16[6144,128]{1,0:T(8,128)(2,1)} async-done(((bf16[768,128]{1,0:T(8,128)(2,1)}), bf16[6144,128]{1,0:T(8,128)(2,1)}) %all-gather.17.cloned.1.call-update) | async-done | bytes 1572880 | tf_op jit(solution)/shard_map/all_gather | solution.py:22
  372.1 3.0 fusion
  375.2 0.4 copy.195
  375.6 25.3 %all_to_all.47 = bf16[4,24,2,32,128]{4,3,2,1,0:T(8,128)(2,1)S(1)} all-to-all(bf16[4,24,2,32,128]{4,3,2,1,0:T(8,128)(2,1)S(1)} %bitcast.118), channel_id=1, replica_groups=mesh['row_0'=4,'row_1'=2,'col'=8,'layer'=4] {'layer'}, dimensions={0} | all-to-all | bytes 3145728 | tf_op jit(solution)/shard_map/all_to_all | solution.py:39
  400.9 0.3 reduce_sum.104
  401.2 17.7 %all_to_all.48 = bf16[24,1,2,32,128]{4,3,2,1,0:T(8,128)(2,1)S(1)} all-to-all(bf16[24,1,2,32,128]{4,3,2,1,0:T(8,128)(2,1)S(1)} %bitcast.127), channel_id=1, replica_groups=mesh['row_0'=4,'row_1'=2,'col'=8,'layer'=4] {'col'}, dimensions={0} | all-to-all | bytes 786432 | tf_op jit(solution)/shard_map/all_to_all | solution.py:95
  418.9 0.8 copy.180
  (49 shorter events, 1.4 us)
Async XLA Ops:
  10.1 43.3 %all-to-all-start.1 = ((bf16[3,8,2,128,128]{4,3,2,0,1:T(8,128)(2,1)}), bf16[3,8,2,128,128]{4,3,2,0,1:T(8,128)(2,1)S(1)}, u32[]{:S(2)}, u32[]{:S(2)}) async-start(bf16[3,8,2,128,128]{4,3,2,0,1:T(8,128)(2,1)} %copy.164), calls=%async_computation.1 | async-start | bytes 3145728 | tf_op jit(solution)/shard_map/all_to_all | solution.py:64
  20.1 107.5 %all-gather.19.cloned.1.call-start = ((), (), s32[]{:S(2)}) async-start(), calls=%async_computation.9 | async-start | bytes 7864320 | tf_op jit(solution)/shard_map/all_gather | solution.py:28
  56.2 142.1 %all-gather.15.cloned.1.call-start = ((), (), s32[]{:S(2)}) async-start(), calls=%async_computation.6 | async-start | bytes 7864320 | tf_op jit(solution)/shard_map/all_gather | solution.py:28
  56.9 147.2 %reduce-scatter.7.cloned.1.call-start = ((), (), s32[]{:S(2)}) async-start(), calls=%async_computation.10 | async-start | bytes 1769472 | tf_op jit(solution)/shard_map/reduce_scatter | solution.py:21
  57.5 194.8 %reduce-scatter.5.cloned.1.call-start = ((), (), s32[]{:S(2)}) async-start(), calls=%async_computation.7 | async-start | bytes 1769472 | tf_op jit(solution)/shard_map/reduce_scatter | solution.py:21
  58.1 221.9 %all-gather.25.cloned.1.call-start = ((), (), s32[]{:S(2)}) async-start(), calls=%async_computation.13 | async-start | bytes 4718592 | tf_op jit(solution)/shard_map/all_gather | solution.py:28
  133.3 170.0 %all-gather.23.cloned.1.call-start = ((), (), s32[]{:S(2)}) async-start(), calls=%async_computation.12 | async-start | bytes 4718592 | tf_op jit(solution)/shard_map/all_gather | solution.py:28
  204.0 0.7 copy-start.1
  204.0 9.2 %copy-start.2 = (u32[256]{0:T(256)S(1)}, u32[256]{0:T(256)}, u32[]{:S(2)}) copy-start(u32[256]{0:T(256)} %constant.104) | copy-start | bytes 3076
  204.0 135.0 %all-gather.21.cloned.1.call-start = ((), (), s32[]{:S(2)}) async-start(), calls=%async_computation.11 | async-start | bytes 1769472 | tf_op jit(solution)/shard_map/all_gather | solution.py:22
  205.4 14.9 %all-to-all-start = ((s32[3,8,2]{0,2,1:T(2,128)}), s32[3,8,2]{0,2,1:T(2,128)S(1)}, u32[]{:S(2)}, u32[]{:S(2)}) async-start(s32[3,8,2]{0,2,1:T(2,128)} %copy.151), calls=%async_computation | async-start | bytes 16384 | tf_op jit(solution)/shard_map/all_to_all | solution.py:65
  213.2 158.9 %all-gather.17.cloned.1.call-start = ((), (), s32[]{:S(2)}) async-start(), calls=%async_computation.8 | async-start | bytes 1769472 | tf_op jit(solution)/shard_map/all_gather | solution.py:22
  339.1 33.1 %copy-start = (bf16[96,128,128]{2,1,0:T(8,128)(2,1)S(1)}, bf16[96,128,128]{2,1,0:T(8,128)(2,1)}, u32[]{:S(2)}) copy-start(bf16[96,128,128]{2,1,0:T(8,128)(2,1)} %gather_fusion.1) | copy-start | bytes 9437188
Sparse Core Ops, SparseCore 0:
  56.3 71.2 all-gather.18
  129.4 68.8 all-gather.14
  200.1 51.0 all-gather.24
  252.9 50.4 all-gather.22
  305.0 33.9 all-gather.20
  340.7 31.3 all-gather.16
Sparse Core Ops, SparseCore 1:
  60.0 43.8 reduce-scatter.6
  106.3 40.2 reduce-scatter.4
